TPU v7x, 32 devices: a whole 2x2x4 slice. The times are simulated.
32 devices in a mesh: fsdp: 8 (over z, x), rep: 4 (over y, core).
Axes of the slice: x: 2, y: 2, z: 4, core: 2. Of those that a mesh axis runs over, the one named last changes fastest.
Arguments:
- cross_base: bfloat16 [4096, 4096], P(('fsdp', 'rep')), may hold values from -6 to 6
- layer_in: bfloat16 [4096, 4096], P(('fsdp', 'rep')), may hold values from -6 to 6
- grad_out: bfloat16 [4096, 4096], P(('fsdp', 'rep')), may hold values from -6 to 6
- reduce_a: bfloat16 [4096, 256], P('fsdp'), may hold values from -0.09375 to 0.09375
- expand_a: bfloat16 [4096, 256], P('fsdp'), may hold values from -0.375 to 0.375
- reduce_b: bfloat16 [4096, 256], P('fsdp'), may hold values from -0.09375 to 0.09375
- expand_b: bfloat16 [4096, 256], P('fsdp'), may hold values from -0.375 to 0.375
Outputs:
- grad_layer_in: bfloat16 [4096, 4096], P(('fsdp', 'rep'))
- grad_base: bfloat16 [4096, 4096], P(('fsdp', 'rep'))
- grad_reduce_a: float32 [4096, 256], P('fsdp')
- grad_expand_a: float32 [4096, 256], P('fsdp')
- grad_reduce_b: float32 [4096, 256], P('fsdp')
- grad_expand_b: float32 [4096, 256], P('fsdp')
All inputs are finite; a program needn't handle non-finite values.
Results may differ from a plain program's by a relative error of at most 0.015.
Values may be sent and summed in bfloat16 or wider, within the bound.
A program may use at most 128 MiB of HBM per device.

v0:
```python
import math

import jax
import jax.numpy as jnp
from jax import lax
from jax.sharding import PartitionSpec as P


def contract_rows(left, right):
    return lax.dot_general(
        left, right, (((0,), (0,)), ((), ())), preferred_element_type=jnp.float32
    )


def contract_cols(left, right):
    return lax.dot_general(
        left, right, (((1,), (1,)), ((), ())), preferred_element_type=jnp.float32
    )


def project(inputs, reduce_full, expand_full):
    narrow = jnp.dot(inputs, reduce_full, preferred_element_type=jnp.float32).astype(jnp.bfloat16)
    return (narrow, contract_cols(narrow, expand_full))


def local_backward(grad_in, cross_base, reduce_full, expand_full):
    grad_wide = grad_in.astype(jnp.float32)
    masked = (grad_wide * cross_base.astype(jnp.float32)).astype(jnp.bfloat16)
    narrow_grad = jnp.dot(masked, expand_full, preferred_element_type=jnp.float32).astype(
        jnp.bfloat16
    )
    passed = grad_wide + contract_cols(narrow_grad, reduce_full)
    return (masked, narrow_grad, passed)


def weight_grads(masked, narrow, inputs, narrow_grad, factor):
    spread = lax.psum_scatter(
        jnp.concatenate(
            (contract_rows(inputs, narrow_grad), contract_rows(masked, narrow)), axis=1
        ),
        ("fsdp", "rep"),
        scatter_dimension=0,
        tiled=True,
    )
    summed = lax.all_gather(spread.astype(jnp.bfloat16), "rep", axis=0, tiled=True).astype(
        spread.dtype
    )
    summed = summed * factor
    rank_width = narrow.shape[1]
    return (summed[:, :rank_width], summed[:, rank_width:])


def on_device(cross_base, layer_in, grad_out, reduce_a, expand_a, reduce_b, expand_b):
    sample_rows = cross_base.shape[0]
    factor = 1.0 / math.sqrt(sample_rows * lax.axis_size("fsdp") * lax.axis_size("rep"))
    reduce_full, expand_full = (
        lax.all_gather(reduce_a, "fsdp", axis=0, tiled=True),
        lax.all_gather(expand_a, "fsdp", axis=0, tiled=True),
    )
    narrow_a, cross_a = project(layer_in, reduce_full, expand_full)
    base_wide = cross_base.astype(jnp.float32)
    middle = (layer_in.astype(jnp.float32) + base_wide * cross_a).astype(jnp.bfloat16)
    top_reduce, top_expand = (
        lax.all_gather(reduce_b, "fsdp", axis=0, tiled=True),
        lax.all_gather(expand_b, "fsdp", axis=0, tiled=True),
    )
    narrow_b, cross_b = project(middle, top_reduce, top_expand)
    masked_b, narrow_grad_b, passed_b = local_backward(grad_out, cross_base, top_reduce, top_expand)
    grad_reduce_b, grad_expand_b = weight_grads(masked_b, narrow_b, middle, narrow_grad_b, factor)
    grad_middle = passed_b.astype(jnp.bfloat16)
    reduce_full, expand_full = (
        lax.all_gather(reduce_a, "fsdp", axis=0, tiled=True),
        lax.all_gather(expand_a, "fsdp", axis=0, tiled=True),
    )
    masked_a, narrow_grad_a, passed_a = local_backward(
        grad_middle, cross_base, reduce_full, expand_full
    )
    grad_reduce_a, grad_expand_a = weight_grads(masked_a, narrow_a, layer_in, narrow_grad_a, factor)
    grad_layer_in = passed_a.astype(jnp.bfloat16)
    grad_base = (
        grad_out.astype(jnp.float32) * cross_b + grad_middle.astype(jnp.float32) * cross_a
    ).astype(jnp.bfloat16)
    return (grad_layer_in, grad_base, grad_reduce_a, grad_expand_a, grad_reduce_b, grad_expand_b)


def solution(mesh):
    placed = (
        P(("fsdp", "rep"), None),
        P(("fsdp", "rep"), None),
        P(("fsdp", "rep"), None),
        P("fsdp", None),
        P("fsdp", None),
        P("fsdp", None),
        P("fsdp", None),
    )
    return jax.shard_map(
        on_device,
        mesh=mesh,
        in_specs=placed,
        out_specs=(
            P(("fsdp", "rep"), None),
            P(("fsdp", "rep"), None),
            P("fsdp", None),
            P("fsdp", None),
            P("fsdp", None),
            P("fsdp", None),
        ),
        check_vma=False,
    )
```

profile of v0, /device:TPU:1, one launch (start us, length us, event | category | flops | bytes accessed | tf_op | source)
XLA Modules:
  0.0 532.9 jit_solution(13636046309037740926)
XLA Ops:
  7.2 0.7 all-gather.11.cloned.1.call-update
  8.0 0.7 all-gather.5.cloned.1.call-update
  8.7 0.7 all-gather.7.cloned.1.call-update
  9.5 0.5 all-gather.9.cloned.1.call-update
  10.0 49.4 %all-gather.11.cloned.1.call-done = bf16[4096,256]{1,0:T(8,128)(2,1)} async-done(((bf16[512,256]{1,0:T(8,128)(2,1)}), bf16[4096,256]{1,0:T(8,128)(2,1)}) %all-gather.11.cloned.1.call-update) | async-done | bytes 2097168 | tf_op jit(solution)/shard_map/all_gather | solution.py:72
  59.4 2.4 convolution_convert_fusion.1
  61.8 47.4 %all-gather.5.cloned.1.call-done = bf16[4096,256]{1,0:T(8,128)(2,1)} async-done(((bf16[512,256]{1,0:T(8,128)(2,1)}), bf16[4096,256]{1,0:T(8,128)(2,1)}) %all-gather.5.cloned.1.call-update) | async-done | bytes 2097168 | tf_op jit(solution)/shard_map/all_gather | solution.py:65
  109.2 2.1 convolution_convert_fusion.3
  111.2 47.7 %all-gather.7.cloned.1.call-done = bf16[4096,256]{1,0:T(8,128)(2,1)} async-done(((bf16[512,256]{1,0:T(8,128)(2,1)}), bf16[4096,256]{1,0:T(8,128)(2,1)}) %all-gather.7.cloned.1.call-update) | async-done | bytes 2097168 | tf_op jit(solution)/shard_map/all_gather | solution.py:64
  158.9 2.7 fusion.2
  161.6 2.7 fusion.12
  164.3 44.3 %all-gather.9.cloned.1.call-done = bf16[4096,256]{1,0:T(8,128)(2,1)} async-done(((bf16[512,256]{1,0:T(8,128)(2,1)}), bf16[4096,256]{1,0:T(8,128)(2,1)}) %all-gather.9.cloned.1.call-update) | async-done | bytes 2097168 | tf_op jit(solution)/shard_map/all_gather | solution.py:73
  208.6 2.1 convolution_convert_fusion.2
  210.7 0.7 convolution_bitcast_fusion
  211.5 1.4 copy-done.1
  212.9 3.8 pad_maximum_fusion
  216.8 4.2 fusion.8
  221.4 0.8 fusion.17
  222.6 0.7 fusion.9
  223.4 3.8 pad_maximum_fusion.1
  227.2 3.6 fusion.3
  230.8 1.9 fusion.4
  232.7 129.9 %reduce-scatter.3.cloned.1.call-done = f32[128,512]{0,1:T(8,128)} async-done(((f32[4096,512]{0,1:T(8,128)}), f32[128,512]{0,1:T(8,128)}) %reduce-scatter.3.cloned.1.call-update) | async-done | bytes 262160 | tf_op jit(solution)/shard_map/reduce_scatter | solution.py:37
  362.6 1.0 convert_element_type.72
  363.6 12.3 %all_gather.24 = bf16[512,512]{0,1:T(8,128)(2,1)S(1)} all-gather(bf16[128,512]{0,1:T(8,128)(2,1)S(1)} %convert_element_type.72), channel_id=1, replica_groups=mesh['fsdp'=8,'rep'=4] {'rep'}, dimensions={0}, use_global_device_ids=true | all-gather | bytes 655360 | tf_op jit(solution)/shard_map/all_gather | solution.py:45
  376.1 1.0 copy.13
  377.1 1.0 copy.14
  378.0 133.3 %reduce-scatter.5.cloned.1.call-done = f32[128,512]{0,1:T(8,128)} async-done(((f32[4096,512]{0,1:T(8,128)}), f32[128,512]{0,1:T(8,128)}) %reduce-scatter.5.cloned.1.call-update) | async-done | bytes 262160 | tf_op jit(solution)/shard_map/reduce_scatter | solution.py:37
  511.3 1.0 convert_element_type.74
  512.3 11.6 %all_gather.25 = bf16[512,512]{0,1:T(8,128)(2,1)S(1)} all-gather(bf16[128,512]{0,1:T(8,128)(2,1)S(1)} %convert_element_type.74), channel_id=1, replica_groups=mesh['fsdp'=8,'rep'=4] {'rep'}, dimensions={0}, use_global_device_ids=true | all-gather | bytes 655360 | tf_op jit(solution)/shard_map/all_gather | solution.py:45
  524.1 1.0 copy.15
  525.1 1.0 copy.16
  (30 shorter events, 1.6 us)
Async XLA Ops:
  7.2 102.0 %copy-start = (bf16[128,4096]{1,0:T(8,128)(2,1)S(1)}, bf16[128,4096]{1,0:T(8,128)(2,1)}, u32[]{:S(2)}) copy-start(bf16[128,4096]{1,0:T(8,128)(2,1)} %param.7) | copy-start | bytes 3145732
  7.2 102.0 %copy-start.2 = (bf16[128,4096]{1,0:T(8,128)(2,1)S(1)}, bf16[128,4096]{1,0:T(8,128)(2,1)}, u32[]{:S(2)}) copy-start(bf16[128,4096]{1,0:T(8,128)(2,1)} %param.9) | copy-start | bytes 3145732
  7.2 52.2 %all-gather.11.cloned.1.call-start = ((), (), s32[]{:S(2)}) async-start(), calls=%async_computation.5 | async-start | bytes 2359296 | tf_op jit(solution)/shard_map/all_gather | solution.py:72
  7.9 101.2 %all-gather.5.cloned.1.call-start = ((), (), s32[]{:S(2)}) async-start(), calls=%async_computation.2 | async-start | bytes 2359296 | tf_op jit(solution)/shard_map/all_gather | solution.py:65
  8.7 150.3 %all-gather.7.cloned.1.call-start = ((), (), s32[]{:S(2)}) async-start(), calls=%async_computation.3 | async-start | bytes 2359296 | tf_op jit(solution)/shard_map/all_gather | solution.py:64
  9.4 199.2 %all-gather.9.cloned.1.call-start = ((), (), s32[]{:S(2)}) async-start(), calls=%async_computation.4 | async-start | bytes 2359296 | tf_op jit(solution)/shard_map/all_gather | solution.py:73
  10.0 352.6 %reduce-scatter.3.cloned.1.call-start = ((), (), s32[]{:S(2)}) async-start(), calls=%async_computation.6 | async-start | bytes 8650752 | tf_op jit(solution)/shard_map/reduce_scatter | solution.py:37
  208.6 2.1 copy-start.5
  210.7 2.2 copy-start.1
  216.7 294.6 %reduce-scatter.5.cloned.1.call-start = ((), (), s32[]{:S(2)}) async-start(), calls=%async_computation.7 | async-start | bytes 8650752 | tf_op jit(solution)/shard_map/reduce_scatter | solution.py:37
  216.8 4.2 copy-start.8
  221.4 1.2 copy-start.3
  227.2 3.6 copy-start.4
  227.2 3.6 copy-start.6
  227.2 3.6 copy-start.7
Sparse Core Ops, SparseCore 0:
  10.1 49.2 all-gather.10
  61.5 47.6 all-gather.4
  111.3 47.6 all-gather.6
  160.9 47.6 all-gather.8
  216.8 145.6 reduce-scatter.2
  364.7 146.5 reduce-scatter.4
where the time goes:
time: 533 us
  waiting for transfers between devices  455 us (85%)
  matrix products  24.2 us (5%)
  blocking collectives  23.9 us (4%)
  between operations  14.3 us (3%)
  other arithmetic  9.73 us (2%)
  local copies, waits for them, and re-layouts  6.07 us (1%)
    reduce_scatter x2, waiting for transfers between devices, weight_grads(): lax.psum_scatter(jnp.concatenate((contract_rows(inputs, narrow_grad), con...  263 us
    all_gather x1, waiting for transfers between devices, on_device(): lax.all_gather(reduce_a, 'fsdp', axis=0, tiled=True)  49.4 us
    all_gather x1, waiting for transfers between devices, on_device(): lax.all_gather(reduce_b, 'fsdp', axis=0, tiled=True)  47.7 us
    all_gather x1, waiting for transfers between devices, on_device(): lax.all_gather(expand_b, 'fsdp', axis=0, tiled=True)  47.4 us
    all_gather x1, waiting for transfers between devices, on_device(): lax.all_gather(expand_a, 'fsdp', axis=0, tiled=True)  44.3 us
    all_gather x2, blocking collectives, weight_grads(): lax.all_gather(spread.astype(jnp.bfloat16), 'rep', axis=0, tiled=True)  23.9 us
    dot_general x4, matrix products, contract_cols(): lax.dot_general(left, right, (((1,), (1,)), ((), ())), preferred_element_...  12.3 us
  transfers between devices with their start and end apart: 6, of which 6 were waited for; matrix products, arithmetic and copies ran while one was open for 5% of the time, Pallas kernels for 0%

commit v1 on v0

v1 whole, which is shorter than its diff:
```python
import functools
import math

import jax
import jax.numpy as jnp
from jax import lax
from jax.experimental import pallas as pl
from jax.experimental.pallas import tpu as pltpu
from jax.sharding import PartitionSpec as P

MESH = pl.DeviceIdType.MESH
F32 = jnp.float32
BF16 = jnp.bfloat16


def dot_nn(left, right):
    return lax.dot_general(left, right, (((1,), (0,)), ((), ())), preferred_element_type=F32)


def dot_nt(left, right):
    return lax.dot_general(left, right, (((1,), (1,)), ((), ())), preferred_element_type=F32)


def dot_tn(left, right):
    return lax.dot_general(left, right, (((0,), (0,)), ((), ())), preferred_element_type=F32)


def kernel(
    F,
    R,
    factor,
    base_in,
    lin_in,
    gout_in,
    ra,
    ea,
    rb,
    eb,
    gli_out,
    gbase_out,
    grads_out,
    base,
    gout,
    own,
    nar,
    peer_wide,
    peer_nar,
    full,
    cross_a,
    gmid,
    gli,
    gbase,
    part,
    grads,
    x1_send,
    x1_recv,
    z1_send,
    z1_recv,
    z2_send,
    z2_recv,
    x2_send,
    x2_recv,
    ybuf,
    load_sem,
    out_sem,
    ag_recv,
    ag_z,
    ag_x,
    ag_d,
    ag_drecv,
    pw_sem,
    pn_sem,
    x1_sem,
    z1_sem,
    z2_sem,
    x2_sem,
    y_ssem,
    y_rsem,
    g_sem,
):
    X = 2
    Z = F // X
    Y = R // 2
    rows = ra.shape[0]
    half = rows // 2
    D = base.shape[1]
    f = lax.axis_index("fsdp")
    r = lax.axis_index("rep")
    z, x = f // X, f % X
    y, c = r // 2, r % 2
    xo = 1 - x
    zp, zm = (z + 1) % Z, (z + Z - 1) % Z

    def dev(ff, rr):
        return {"fsdp": ff, "rep": rr}

    up, down = dev(zp * X + x, r), dev(zm * X + x, r)
    across = dev(z * X + xo, r)
    mate = dev(f, y * 2 + 1 - c)

    def ymate(i):
        return dev(f, ((y + i) % Y) * 2 + c)

    loads = []
    for i, (src, dst) in enumerate(
        (
            (ra, full.at[0, pl.ds(pl.multiple_of(f * rows, rows), rows), :]),
            (ea, full.at[1, pl.ds(pl.multiple_of(f * rows, rows), rows), :]),
            (rb, full.at[2, pl.ds(pl.multiple_of(f * rows, rows), rows), :]),
            (eb, full.at[3, pl.ds(pl.multiple_of(f * rows, rows), rows), :]),
            (base_in, base),
            (gout_in, gout),
            (lin_in, own.at[0, 0]),
        )
    ):
        copy = pltpu.make_async_copy(src, dst, load_sem.at[i])
        copy.start()
        loads.append(copy)

    barrier = pltpu.get_barrier_semaphore()
    friends = [up, down, across, mate] + [ymate(i) for i in range(1, Y)]
    for friend in friends:
        pl.semaphore_signal(barrier, inc=1, device_id=friend, device_id_type=MESH)
    pl.semaphore_wait(barrier, len(friends))
    for copy in loads[:4]:
        copy.wait()

    def piece(w, zz, xx, h):
        start = ((zz + 2 * Z) % Z * X + xx) * rows + h * half
        return full.at[w, pl.ds(pl.multiple_of(start, half), half), :]

    def slot(zz, xx):
        return (zz + 2 * Z) % Z * X + xx

    sent = []

    def send(ref, ssem, rsem, target):
        copy = pltpu.make_async_remote_copy(
            src_ref=ref, dst_ref=ref, send_sem=ssem, recv_sem=rsem,
            device_id=target, device_id_type=MESH,
        )
        copy.start()
        sent.append(copy)

    def zsend(k, zz, xx, h):
        o = slot(zz, xx)
        send(piece(2 * c + k, zz, xx, h), ag_z.at[k, o, h], ag_recv.at[k, o, h], down if h else up)

    def xsend(k, zz, xx, h):
        o = slot(zz, xx)
        send(piece(2 * c + k, zz, xx, h), ag_x.at[k, o, h], ag_recv.at[k, o, h], across)

    def dsend(k, zz, xx, h):
        o = slot(zz, xx)
        send(piece(2 * c + k, zz, xx, h), ag_d.at[k, o, h], ag_drecv.at[k, o, h], mate)

    def arrive(k, zz, xx, h):
        o = slot(zz, xx)
        ref = piece(2 * c + k, zz, xx, h)
        pltpu.make_async_remote_copy(
            src_ref=ref, dst_ref=ref, send_sem=ag_z.at[k, o, h], recv_sem=ag_recv.at[k, o, h],
            device_id=up, device_id_type=MESH,
        ).wait_recv()

    for h in range(2):
        zsend(1, z, x, h)
        xsend(0, z, x, h)
    for h in range(2):
        zsend(0, z, x, h)
        xsend(1, z, x, h)

    for copy in loads[4:]:
        copy.wait()
    tile = min(512, D)

    @pl.loop(0, D // tile)
    def _(t):
        cols = pl.ds(pl.multiple_of(t * tile, tile), tile)
        own[1, 1, :, cols] = (gout[:, cols].astype(F32) * base[:, cols].astype(F32)).astype(BF16)

    for s in range(1, Z + 1):
        for h in range(2):
            sign = 1 if h else -1
            if s < Z:
                zz = z + sign * s
                arrive(1, zz, x, h)
                if s < Z - 1:
                    zsend(1, zz, x, h)
                xsend(1, zz, x, h)
                dsend(1, zz, x, h)
            zo = z + sign * (s - 1)
            arrive(0, zo, xo, h)
            if s < Z:
                zsend(0, zo, xo, h)
            dsend(0, zo, xo, h)
            if s < Z:
                zz = z + sign * s
                arrive(0, zz, x, h)
                if s < Z - 1:
                    zsend(0, zz, x, h)
                dsend(0, zz, x, h)
        for h in range(2):
            sign = 1 if h else -1
            zo = z + sign * (s - 1)
            arrive(1, zo, xo, h)
            dsend(1, zo, xo, h)
    for k in range(2):
        for s in range(Z):
            for xx in (x, xo):
                if s == 0 and xx is x:
                    continue
                for h in range(2):
                    zz = z + (s if h else -s)
                    o = slot(zz, xx)
                    ref = piece(2 * (1 - c) + k, zz, xx, h)
                    pltpu.make_async_remote_copy(
                        src_ref=ref, dst_ref=ref, send_sem=ag_d.at[k, o, h],
                        recv_sem=ag_drecv.at[k, o, h], device_id=mate, device_id_type=MESH,
                    ).wait_recv()
    for copy in sent:
        copy.wait_send()

    nar[0, 1] = dot_nn(own[0, 0], full[0]).astype(BF16)
    nar[1, 0] = dot_nn(own[1, 1], full[3]).astype(BF16)

    @pl.loop(0, D // tile)
    def _(t):
        cols = pl.ds(pl.multiple_of(t * tile, tile), tile)
        wide = base[:, cols].astype(F32)
        crossed = dot_nt(nar[0, 1], full[1, cols, :])
        cross_a[:, cols] = crossed
        own[1, 0, :, cols] = (own[0, 0, :, cols].astype(F32) + wide * crossed).astype(BF16)
        passed = (gout[:, cols].astype(F32) + dot_nt(nar[1, 0], full[2, cols, :])).astype(BF16)
        gmid[:, cols] = passed
        own[0, 1, :, cols] = (passed.astype(F32) * wide).astype(BF16)

    nar[1, 1] = dot_nn(own[1, 0], full[2]).astype(BF16)
    nar[0, 0] = dot_nn(own[0, 1], full[1]).astype(BF16)

    swaps = []
    for k in range(2):
        for src, dst, sem in ((own, peer_wide, pw_sem), (nar, peer_nar, pn_sem)):
            copy = pltpu.make_async_remote_copy(
                src_ref=src.at[1 - c, k], dst_ref=dst.at[k], send_sem=sem.at[0, k],
                recv_sem=sem.at[1, k], device_id=mate, device_id_type=MESH,
            )
            copy.start()
            swaps.append(copy)

    def push(src, dst, sems, target):
        copy = pltpu.make_async_remote_copy(
            src_ref=src, dst_ref=dst, send_sem=sems[0], recv_sem=sems[1],
            device_id=target, device_id_type=MESH,
        )
        copy.start()
        return copy

    for copy in swaps:
        copy.wait()

    @pl.loop(0, D // tile)
    def _(t):
        cols = pl.ds(pl.multiple_of(t * tile, tile), tile)
        for k in range(2):
            part[k, cols, :] = dot_tn(own[c, k, :, cols], nar[c, k]) + dot_tn(
                peer_wide[k, :, cols], peer_nar[k]
            )

    def mine(k, zz, xx, h=None):
        start = slot(zz, xx) * rows
        if h is None:
            return part[k, pl.ds(pl.multiple_of(start, rows), rows), :]
        return part[k, pl.ds(pl.multiple_of(start + h * half, half), half), :]

    hx1, hz1, hz2 = {}, {}, {}

    def send_z2(s):
        for h in range(2):
            zz = z + (1 + s) * (1 if h else -1)
            for i, xx in enumerate((x, xo)):
                value = mine(1, zz, xx, h)
                if s > 0:
                    hz2[s - 1, h, i].wait_recv()
                    value = value + z2_recv[s - 1, h, i].astype(F32)
                z2_send[s, h, i] = value.astype(BF16)
                hz2[s, h, i] = push(
                    z2_send.at[s, h, i], z2_recv.at[s, h, i],
                    (z2_sem.at[0, s, h, i], z2_sem.at[1, s, h, i]), down if h else up,
                )

    def send_z1(s):
        for h in range(2):
            zz = z + (1 + s) * (1 if h else -1)
            value = mine(0, zz, x, h)
            value = value + x1_recv[(zz + 2 * Z) % Z, pl.ds(h * half, half), :].astype(F32)
            if s > 0:
                hz1[s - 1, h].wait_recv()
                value = value + z1_recv[s - 1, h].astype(F32)
            z1_send[s, h] = value.astype(BF16)
            hz1[s, h] = push(
                z1_send.at[s, h], z1_recv.at[s, h],
                (z1_sem.at[0, s, h], z1_sem.at[1, s, h]), down if h else up,
            )

    send_z2(0)
    order = []
    for d in range(1, Z):
        order.append(d // 2 + 1 if d % 2 else -(d // 2))
    order.append(0)
    for i, d in enumerate(order):
        zz = (z + d + 2 * Z) % Z
        x1_send[zz] = mine(0, zz, xo).astype(BF16)
        hx1[i] = push(
            x1_send.at[zz], x1_recv.at[zz], (x1_sem.at[0, zz], x1_sem.at[1, zz]), across
        )

    @pl.loop(0, D // tile)
    def _(t):
        cols = pl.ds(pl.multiple_of(t * tile, tile), tile)
        held = gmid[:, cols].astype(F32)
        crossed = dot_nt(nar[1, 1], full[3, cols, :])
        gbase[:, cols] = (gout[:, cols].astype(F32) * crossed + held * cross_a[:, cols]).astype(BF16)
        gli[:, cols] = (held + dot_nt(nar[0, 0], full[0, cols, :])).astype(BF16)

    outs = []
    for i, (src, dst) in enumerate(((gli, gli_out), (gbase, gbase_out))):
        copy = pltpu.make_async_copy(src, dst, out_sem.at[i])
        copy.start()
        outs.append(copy)

    for s in range(1, Z - 1):
        send_z2(s)
    for h in range(2):
        for i in range(2):
            hz2[Z - 2, h, i].wait_recv()
    for h in range(2):
        x2_send[pl.ds(h * half, half), :] = (
            mine(1, z, xo, h) + z2_recv[Z - 2, h, 1].astype(F32)
        ).astype(BF16)
    hx2 = push(x2_send, x2_recv, (x2_sem.at[0], x2_sem.at[1]), across)
    for i in range(Z):
        hx1[i].wait_recv()
    for s in range(Z - 1):
        send_z1(s)

    hy = []

    def send_y(k):
        for i in range(1, Y):
            hy.append(
                push(ybuf.at[k, y], ybuf.at[k, y], (y_ssem.at[k, i], y_rsem.at[k, i]), ymate(i))
            )

    hx2.wait_recv()
    for h in range(2):
        ybuf[1, y, pl.ds(h * half, half), :] = (
            mine(1, z, x, h)
            + z2_recv[Z - 2, h, 0].astype(F32)
            + x2_recv[pl.ds(h * half, half), :].astype(F32)
        ).astype(BF16)
    send_y(1)
    for h in range(2):
        hz1[Z - 2, h].wait_recv()
        ybuf[0, y, pl.ds(h * half, half), :] = (
            mine(0, z, x, h)
            + x1_recv[z, pl.ds(h * half, half), :].astype(F32)
            + z1_recv[Z - 2, h].astype(F32)
        ).astype(BF16)
    send_y(0)
    hg = []
    for j, k in enumerate((1, 0)):
        for i in range(Y - 1):
            from_y = (y + Y - (i + 1)) % Y
            pltpu.make_async_remote_copy(
                src_ref=ybuf.at[k, from_y], dst_ref=ybuf.at[k, from_y],
                send_sem=y_ssem.at[k, i + 1], recv_sem=y_rsem.at[k, i + 1],
                device_id=ymate(i + 1), device_id_type=MESH,
            ).wait_recv()
        total = ybuf[k, 0].astype(F32)
        for i in range(1, Y):
            total = total + ybuf[k, i].astype(F32)
        grads[2 * c + k] = total * factor
        hg.append(
            push(grads.at[2 * c + k], grads.at[2 * c + k], (g_sem.at[0, k], g_sem.at[1, k]), mate)
        )
    for k in range(2):
        w = 2 * (1 - c) + k
        pltpu.make_async_remote_copy(
            src_ref=grads.at[w], dst_ref=grads.at[w], send_sem=g_sem.at[0, k],
            recv_sem=g_sem.at[1, k], device_id=mate, device_id_type=MESH,
        ).wait_recv()
    last = pltpu.make_async_copy(grads, grads_out, out_sem.at[2])
    last.start()
    for copy in list(hx1.values()) + list(hz1.values()) + list(hz2.values()) + [hx2] + hy + hg:
        copy.wait_send()
    for copy in outs + [last]:
        copy.wait()


def solution(mesh):
    F, R = mesh.shape["fsdp"], mesh.shape["rep"]
    X = 2
    Z, Y = F // X, R // 2

    def on_device(base, lin, gout, ra, ea, rb, eb):
        T, D = base.shape
        rows, K = ra.shape
        half = rows // 2
        factor = 1.0 / math.sqrt(T * F * R)
        dma = pltpu.SemaphoreType.DMA
        vm = pltpu.VMEM
        any_spec = pl.BlockSpec(memory_space=pl.ANY)
        gli, gbase, grads = pl.pallas_call(
            functools.partial(kernel, F, R, factor),
            out_shape=(
                jax.ShapeDtypeStruct((T, D), BF16),
                jax.ShapeDtypeStruct((T, D), BF16),
                jax.ShapeDtypeStruct((4, rows, K), F32),
            ),
            in_specs=[any_spec] * 7,
            out_specs=[any_spec] * 3,
            scratch_shapes=[
                vm((T, D), BF16),
                vm((T, D), BF16),
                vm((2, 2, T, D), BF16),
                vm((2, 2, T, K), BF16),
                vm((2, T, D), BF16),
                vm((2, T, K), BF16),
                vm((4, D, K), BF16),
                vm((T, D), F32),
                vm((T, D), BF16),
                vm((T, D), BF16),
                vm((T, D), BF16),
                vm((2, D, K), F32),
                vm((4, rows, K), F32),
                vm((Z, rows, K), BF16),
                vm((Z, rows, K), BF16),
                vm((Z - 1, 2, half, K), BF16),
                vm((Z - 1, 2, half, K), BF16),
                vm((Z - 1, 2, 2, half, K), BF16),
                vm((Z - 1, 2, 2, half, K), BF16),
                vm((rows, K), BF16),
                vm((rows, K), BF16),
                vm((2, Y, rows, K), BF16),
                dma((7,)),
                dma((3,)),
                dma((2, F, 2)),
                dma((2, F, 2)),
                dma((2, F, 2)),
                dma((2, F, 2)),
                dma((2, F, 2)),
                dma((2, 2)),
                dma((2, 2)),
                dma((2, Z)),
                dma((2, Z - 1, 2)),
                dma((2, Z - 1, 2, 2)),
                dma((2,)),
                dma((2, Y)),
                dma((2, Y)),
                dma((2, 2)),
            ],
            compiler_params=pltpu.CompilerParams(
                collective_id=1, has_side_effects=True, vmem_limit_bytes=60 * 1024 * 1024
            ),
        )(base, lin, gout, ra, ea, rb, eb)
        return gli, gbase, grads[0], grads[1], grads[2], grads[3]

    both = P(("fsdp", "rep"), None)
    one = P("fsdp", None)
    return jax.shard_map(
        on_device,
        mesh=mesh,
        in_specs=(both, both, both, one, one, one, one),
        out_specs=(both, both, one, one, one, one),
        check_vma=False,
    )
```

time: 533 us -> 146 us (0.27)
  waiting for transfers between devices: 455 us -> 0 us
  Pallas kernels: 0 us -> 140 us
  matrix products: 24.2 us -> 0 us
  blocking collectives: 23.9 us -> 0 us
  between operations: 14.3 us -> 0.65 us
  other arithmetic: 9.73 us -> 0 us
    reduce_scatter x2 -> x0, waiting for transfers between devices: 263 us -> none  [weight_grads(): lax.psum_scatter(jnp.concatenate((contract_rows(inputs, narrow_grad), con...]
    all_gather x4 -> x0, waiting for transfers between devices: 189 us -> none  [the longest x1 49.4 us: on_device(): lax.all_gather(reduce_a, 'fsdp', axis=0, tiled=True)]
    pallas_call x0 -> x1, Pallas kernels: none -> 140 us  [on_device(): pl.pallas_call(functools.partial(kernel, F, R, factor), out_shape=(jax.Sh...]
    dot_general x12 -> x0, matrix products: 24.2 us -> none  [the longest x4 12.3 us: contract_cols(): lax.dot_general(left, right, (((1,), (1,)), ((), ())), preferred_element_...]
    all_gather x2 -> x0, blocking collectives: 23.9 us -> none  [weight_grads(): lax.all_gather(spread.astype(jnp.bfloat16), 'rep', axis=0, tiled=True)]
    concatenate x2 -> x0, other arithmetic: 7.55 us -> none  [weight_grads(): jnp.concatenate((contract_rows(inputs, narrow_grad), contract_rows(masked...]
  transfers between devices with their start and end apart: 6 -> 0, of which waited for: 6 -> 0; matrix products, arithmetic and copies ran while one was open for 5% -> 0% of each run, Pallas kernels for 0% -> 0%
where the time goes in v1:
time: 146 us
  Pallas kernels  140 us (96%)
  local copies, waits for them, and re-layouts  5.52 us (4%)
    pallas_call x1, Pallas kernels, on_device(): pl.pallas_call(functools.partial(kernel, F, R, factor), out_shape=(jax.Sh...  140 us
    squeeze x1, local copies, waits for them, and re-layouts, on_device(): return (gli, gbase, grads[0], grads[1], grads[2], grads[3])  2.95 us

profile of v1, /device:TPU:1, one launch (start us, length us, event | category | flops | bytes accessed | tf_op | source)
XLA Modules:
  0.0 145.8 jit_solution(2863608529419922653)
XLA Ops:
  0.6 139.6 %shard_map.118 = (bf16[128,4096]{1,0:T(8,128)(2,1)}, bf16[128,4096]{1,0:T(8,128)(2,1)}, f32[4,512,256]{2,1,0:T(8,128)}) custom-call(bf16[128,4096]{1,0:T(8,128)(2,1)} %base_in.1, bf16[128,4096]{1,0:T(8,128)(2,1)} %lin_in.1, bf16[128,4096]{1,0:T(8,128)(2,1)} %gout_in.1, bf16[512,256]{1,0:T(8,128)(2,1)} %ra.1, bf16[512,256]{1,0:T(8,128)(2,1)} %ea.1, ...), custom_call_target="tpu_custom_call" | custom-call | tf_op jit(solution)/shard_map/pallas_call | solution.py:413
  140.2 0.0 copy-start.1
  140.2 2.9 %slice_bitcast_fusion = (f32[512,256]{1,0:T(8,128)}, f32[512,256]{1,0:T(8,128)}, f32[512,256]{1,0:T(8,128)}, f32[512,256]{1,0:T(8,128)}) fusion(f32[4,512,256]{2,1,0:T(8,128)} %get-tuple-element.11), kind=kLoop, calls=%fused_computation | loop fusion | bytes 4194304 | tf_op jit(solution)/shard_map/squeeze | solution.py:466
  143.2 0.0 copy-start
  143.2 0.0 copy-done.1
  143.2 1.0 copy.15
  144.2 0.6 copy-done
  144.8 1.0 copy.16
Async XLA Ops:
  140.2 3.0 %copy-start.1 = (bf16[128,4096]{1,0:T(8,128)(2,1)S(1)}, bf16[128,4096]{1,0:T(8,128)(2,1)}, u32[]{:S(2)}) copy-start(bf16[128,4096]{1,0:T(8,128)(2,1)} %get-tuple-element.22) | copy-start | bytes 3145732
  143.2 1.6 %copy-start = (bf16[128,4096]{1,0:T(8,128)(2,1)S(1)}, bf16[128,4096]{1,0:T(8,128)(2,1)}, u32[]{:S(2)}) copy-start(bf16[128,4096]{1,0:T(8,128)(2,1)} %get-tuple-element.23) | copy-start | bytes 3145732

commit v2 on v1

v2 whole, which is shorter than its diff:
```python
import functools
import math

import jax
import jax.numpy as jnp
from jax import lax
from jax.experimental import pallas as pl
from jax.experimental.pallas import tpu as pltpu
from jax.sharding import PartitionSpec as P

MESH = pl.DeviceIdType.MESH
F32 = jnp.float32
BF16 = jnp.bfloat16


def dot_nn(left, right):
    return lax.dot_general(left, right, (((1,), (0,)), ((), ())), preferred_element_type=F32)


def dot_nt(left, right):
    return lax.dot_general(left, right, (((1,), (1,)), ((), ())), preferred_element_type=F32)


def dot_tn(left, right):
    return lax.dot_general(left, right, (((0,), (0,)), ((), ())), preferred_element_type=F32)


def kernel(
    F,
    R,
    factor,
    base_in,
    lin_in,
    gout_in,
    ra,
    ea,
    rb,
    eb,
    gli_out,
    gbase_out,
    grads_out,
    base,
    gout,
    own,
    nar,
    peer_wide,
    peer_nar,
    full,
    cross_a,
    gmid,
    gli,
    gbase,
    part,
    grads,
    y1_send,
    y1_recv,
    x1_send,
    x1_recv,
    x2_send,
    x2_recv,
    y2_send,
    y2_recv,
    z_send,
    z_recv,
    last_sum,
    fin,
    load_sem,
    out_sem,
    ag_recv,
    ag_z,
    ag_x,
    ag_y,
    ag_d,
    ag_drecv,
    pw_sem,
    pn_sem,
    y1_sem,
    x1_sem,
    x2_sem,
    y2_sem,
    zs_sem,
    zr_sem,
    y_ssem,
    y_rsem,
    g_sem,
):
    X = 2
    Z = F // X
    rows = ra.shape[0]
    half = rows // 2
    D = base.shape[1]
    f = lax.axis_index("fsdp")
    r = lax.axis_index("rep")
    z, x = f // X, f % X
    y, c = r // 2, r % 2
    xo = 1 - x
    zp, zm = (z + 1) % Z, (z + Z - 1) % Z

    def dev(ff, rr):
        return {"fsdp": ff, "rep": rr}

    up, down = dev(zp * X + x, r), dev(zm * X + x, r)
    across = dev(z * X + xo, r)
    mate = dev(f, y * 2 + 1 - c)

    twin = dev(f, (1 - y) * 2 + c)

    loads = []
    for i, (src, dst) in enumerate(
        (
            (ra, full.at[0, pl.ds(pl.multiple_of(f * rows, rows), rows), :]),
            (ea, full.at[1, pl.ds(pl.multiple_of(f * rows, rows), rows), :]),
            (rb, full.at[2, pl.ds(pl.multiple_of(f * rows, rows), rows), :]),
            (eb, full.at[3, pl.ds(pl.multiple_of(f * rows, rows), rows), :]),
            (base_in, base),
            (gout_in, gout),
            (lin_in, own.at[0, 0]),
        )
    ):
        copy = pltpu.make_async_copy(src, dst, load_sem.at[i])
        copy.start()
        loads.append(copy)

    barrier = pltpu.get_barrier_semaphore()
    friends = [up, down, across, mate, twin]
    for friend in friends:
        pl.semaphore_signal(barrier, inc=1, device_id=friend, device_id_type=MESH)
    pl.semaphore_wait(barrier, len(friends))
    for copy in loads[:4]:
        copy.wait()

    sent = []

    def guarded(cond, action):
        if cond is None:
            action()
        else:
            pl.when(cond)(action)

    def also(one, two):
        return one if two is None else two if one is None else jnp.logical_and(one, two)

    def slot(zz, xx):
        return (zz + 2 * Z) % Z * X + xx

    def piece(w, zz, xx, h):
        start = slot(zz, xx) * rows + h * half
        return full.at[w, pl.ds(pl.multiple_of(start, half), half), :]

    def relay(cond, k, zz, xx, h, ssem, rsem, target):
        ref = piece(2 * c + k, zz, xx, h)
        copy = pltpu.make_async_remote_copy(
            src_ref=ref, dst_ref=ref, send_sem=ssem, recv_sem=rsem,
            device_id=target, device_id_type=MESH,
        )
        guarded(cond, copy.start)
        sent.append((cond, copy))

    def zsend(cond, zz, h, upward):
        o = slot(zz, x)
        relay(cond, y, zz, x, h, ag_z.at[upward, o, h], ag_recv.at[y, o, h], up if upward else down)

    def xsend(cond, k, zz, h):
        o = slot(zz, x)
        relay(cond, k, zz, x, h, ag_x.at[k, o, h], ag_recv.at[k, o, h], across)

    def ysend(cond, zz, xx, h):
        o = slot(zz, xx)
        relay(cond, y, zz, xx, h, ag_y.at[y, o, h], ag_recv.at[y, o, h], twin)

    def dsend(cond, k, zz, xx, h):
        o = slot(zz, xx)
        relay(cond, k, zz, xx, h, ag_d.at[k, o, h], ag_drecv.at[k, o, h], mate)

    def arrive(cond, k, zz, xx, h):
        o = slot(zz, xx)
        ref = piece(2 * c + k, zz, xx, h)
        copy = pltpu.make_async_remote_copy(
            src_ref=ref, dst_ref=ref, send_sem=ag_d.at[k, o, h], recv_sem=ag_recv.at[k, o, h],
            device_id=mate, device_id_type=MESH,
        )
        guarded(cond, copy.wait_recv)

    def levels(d):
        if d < 0 or d >= Z:
            return []
        if d == 0:
            return [(z, None, None)]
        return [(z - d, z >= d, True), (z + d, z + d < Z, False)]

    not_top, not_bottom = z < Z - 1, z > 0
    yo = 1 - y

    def stage_line(d):
        for h in range(2):
            for zz, cond, upward in levels(d):
                if d == 0:
                    zsend(not_top, zz, h, 1)
                    zsend(not_bottom, zz, h, 0)
                else:
                    arrive(cond, y, zz, x, h)
                    if d < Z - 1:
                        zsend(also(cond, not_top if upward else not_bottom), zz, h, 1 if upward else 0)
                xsend(cond, y, zz, h)
                if d == 0:
                    if h == 1:
                        xsend(cond, yo, zz, h)
                else:
                    ysend(cond, zz, x, h)
                    dsend(cond, y, zz, x, h)

    def stage_side(d):
        for h in range(2):
            for zz, cond, _ in levels(d):
                arrive(cond, y, zz, xo, h)
                if h == 0:
                    ysend(cond, zz, xo, h)
                dsend(cond, y, zz, xo, h)
                if d > 0:
                    arrive(cond, yo, zz, x, h)
                    if h == 1:
                        xsend(cond, yo, zz, h)
                    dsend(cond, yo, zz, x, h)

    def stage_corner(d):
        for h in range(2):
            for zz, cond, _ in levels(d):
                arrive(cond, yo, zz, xo, h)
                dsend(cond, yo, zz, xo, h)

    stage_line(0)

    for copy in loads[4:]:
        copy.wait()
    tile = min(512, D)

    @pl.loop(0, D // tile)
    def _(t):
        cols = pl.ds(pl.multiple_of(t * tile, tile), tile)
        own[1, 1, :, cols] = (gout[:, cols].astype(F32) * base[:, cols].astype(F32)).astype(BF16)

    for d in range(1, Z + 2):
        if d < Z:
            stage_line(d)
        stage_side(d - 1)
        stage_corner(d - 2)
    for d in range(Z):
        for zz, cond, _ in levels(d):
            for k in range(2):
                for h in range(2):
                    for near in (True, False):
                        if near and d == 0:
                            continue
                        xx = x if near else xo
                        o = slot(zz, xx)
                        ref = piece(2 * (1 - c) + k, zz, xx, h)
                        copy = pltpu.make_async_remote_copy(
                            src_ref=ref, dst_ref=ref, send_sem=ag_d.at[k, o, h],
                            recv_sem=ag_drecv.at[k, o, h], device_id=mate, device_id_type=MESH,
                        )
                        guarded(cond, copy.wait_recv)
    for cond, copy in sent:
        guarded(cond, copy.wait_send)

    nar[0, 1] = dot_nn(own[0, 0], full[0]).astype(BF16)
    nar[1, 0] = dot_nn(own[1, 1], full[3]).astype(BF16)

    @pl.loop(0, D // tile)
    def _(t):
        cols = pl.ds(pl.multiple_of(t * tile, tile), tile)
        wide = base[:, cols].astype(F32)
        crossed = dot_nt(nar[0, 1], full[1, cols, :])
        cross_a[:, cols] = crossed
        own[1, 0, :, cols] = (own[0, 0, :, cols].astype(F32) + wide * crossed).astype(BF16)
        passed = (gout[:, cols].astype(F32) + dot_nt(nar[1, 0], full[2, cols, :])).astype(BF16)
        gmid[:, cols] = passed
        own[0, 1, :, cols] = (passed.astype(F32) * wide).astype(BF16)

    nar[1, 1] = dot_nn(own[1, 0], full[2]).astype(BF16)
    nar[0, 0] = dot_nn(own[0, 1], full[1]).astype(BF16)

    swaps = []
    for k in range(2):
        for src, dst, sem in ((own, peer_wide, pw_sem), (nar, peer_nar, pn_sem)):
            copy = pltpu.make_async_remote_copy(
                src_ref=src.at[1 - c, k], dst_ref=dst.at[k], send_sem=sem.at[0, k],
                recv_sem=sem.at[1, k], device_id=mate, device_id_type=MESH,
            )
            copy.start()
            swaps.append(copy)

    def push(src, dst, sems, target):
        copy = pltpu.make_async_remote_copy(
            src_ref=src, dst_ref=dst, send_sem=sems[0], recv_sem=sems[1],
            device_id=target, device_id_type=MESH,
        )
        copy.start()
        return copy

    for copy in swaps:
        copy.wait()
    level_rows = X * rows

    def products(o):
        cols = pl.ds(pl.multiple_of(o * level_rows, level_rows), level_rows)
        for k in range(2):
            part[k, cols, :] = dot_tn(own[c, k, :, cols], nar[c, k]) + dot_tn(
                peer_wide[k, :, cols], peer_nar[k]
            )

    def mine(k, o, xx, h):
        start = (o * X + xx) * rows + h * half
        return part[k, pl.ds(pl.multiple_of(start, half), half), :]

    flipped = z >= Z // 2
    near_end = jnp.where(flipped, Z - 1 - z, z)

    def owner(i):
        if i == Z - 1:
            return z
        j = Z - 1 - i
        o = jnp.where(j > near_end, j, j - 1)
        return jnp.where(flipped, Z - 1 - o, o)

    sums, waits = [], []

    def first(i):
        o = owner(i)
        products(o)
        for xx in range(2):
            y1_send[o, xx] = mine(yo, o, xx, 0).astype(BF16)
        one = push(y1_send.at[o], y1_recv.at[o], (y1_sem.at[0, o], y1_sem.at[1, o]), twin)
        for k in range(2):
            x1_send[o, k] = mine(k, o, xo, 1).astype(BF16)
        two = push(x1_send.at[o], x1_recv.at[o], (x1_sem.at[0, o], x1_sem.at[1, o]), across)
        waits.extend((one, two))
        sums.append([one, two])

    def second(i):
        o = owner(i)
        one, two = sums[i]
        one.wait_recv()
        x2_send[o] = (mine(y, o, xo, 0) + y1_recv[o, xo].astype(F32)).astype(BF16)
        three = push(x2_send.at[o], x2_recv.at[o], (x2_sem.at[0, o], x2_sem.at[1, o]), across)
        two.wait_recv()
        y2_send[o] = (mine(yo, o, x, 1) + x1_recv[o, yo].astype(F32)).astype(BF16)
        four = push(y2_send.at[o], y2_recv.at[o], (y2_sem.at[0, o], y2_sem.at[1, o]), twin)
        waits.extend((three, four))
        sums[i] = (three, four)

    def level_sum(o, h):
        if h == 0:
            return mine(y, o, x, 0) + y1_recv[o, x].astype(F32) + x2_recv[o].astype(F32)
        return mine(y, o, x, 1) + x1_recv[o, y].astype(F32) + y2_recv[o].astype(F32)

    def line(o, h, way, target):
        return pltpu.make_async_remote_copy(
            src_ref=z_send.at[o, h], dst_ref=z_recv.at[way, o, h], send_sem=zs_sem.at[o, h],
            recv_sem=zr_sem.at[way, o, h], device_id=target, device_id_type=MESH,
        )

    def third(i):
        o = owner(i)
        way = jnp.where(o > z, 0, 1)
        target = dev((z + 1 - 2 * way) * X + x, r)
        fed = jnp.where(o > z, z, Z - 1 - z) > 0
        for h in range(2):
            sums[i][h].wait_recv()
            value = level_sum(o, h)
            copy = line(o, h, way, target)

            @pl.when(fed)
            def _():
                copy.wait_recv()
                z_send[o, h] = (value + z_recv[way, o, h].astype(F32)).astype(BF16)

            @pl.when(jnp.logical_not(fed))
            def _():
                z_send[o, h] = value.astype(BF16)

            copy.start()
            waits.append(copy)

    def others():
        @pl.loop(0, D // tile)
        def _(t):
            cols = pl.ds(pl.multiple_of(t * tile, tile), tile)
            held = gmid[:, cols].astype(F32)
            crossed = dot_nt(nar[1, 1], full[3, cols, :])
            gbase[:, cols] = (
                gout[:, cols].astype(F32) * crossed + held * cross_a[:, cols]
            ).astype(BF16)
            gli[:, cols] = (held + dot_nt(nar[0, 0], full[0, cols, :])).astype(BF16)

    outs = []
    for i in range(Z + 1):
        if i < Z:
            first(i)
        if i == min(1, Z - 1):
            others()
            for n, (src, dst) in enumerate(((gli, gli_out), (gbase, gbase_out))):
                copy = pltpu.make_async_copy(src, dst, out_sem.at[n])
                copy.start()
                outs.append(copy)
        if 1 <= i:
            second(i - 1)
        if 2 <= i:
            third(i - 2)

    hy = []
    for h in range(2):
        sums[Z - 1][h].wait_recv()
        last_sum[h] = level_sum(z, h)
        for way, cond in ((0, not_bottom), (1, not_top)):

            @pl.when(cond)
            def _():
                line(z, h, way, across).wait_recv()
                last_sum[h] = last_sum[h] + z_recv[way, z, h].astype(F32)

        fin[y, h] = last_sum[h].astype(BF16)
        hy.append(push(fin.at[y, h], fin.at[y, h], (y_ssem.at[y, h], y_rsem.at[y, h]), twin))
    hg = []

    def hand_over(k, h):
        grads[2 * c + k, pl.ds(h * half, half), :] = fin[k, h].astype(F32) * factor
        ref = grads.at[2 * c + k, pl.ds(h * half, half), :]
        hg.append(push(ref, ref, (g_sem.at[0, k, h], g_sem.at[1, k, h]), mate))

    for h in range(2):
        hand_over(y, h)
    for h in range(2):
        pltpu.make_async_remote_copy(
            src_ref=fin.at[yo, h], dst_ref=fin.at[yo, h], send_sem=y_ssem.at[yo, h],
            recv_sem=y_rsem.at[yo, h], device_id=twin, device_id_type=MESH,
        ).wait_recv()
        hand_over(yo, h)
    for k in range(2):
        for h in range(2):
            ref = grads.at[2 * (1 - c) + k, pl.ds(h * half, half), :]
            pltpu.make_async_remote_copy(
                src_ref=ref, dst_ref=ref, send_sem=g_sem.at[0, k, h],
                recv_sem=g_sem.at[1, k, h], device_id=mate, device_id_type=MESH,
            ).wait_recv()
    last = pltpu.make_async_copy(grads, grads_out, out_sem.at[2])
    last.start()
    for copy in waits + hy + hg:
        copy.wait_send()
    for copy in outs + [last]:
        copy.wait()


def solution(mesh):
    F, R = mesh.shape["fsdp"], mesh.shape["rep"]
    X = 2
    Z = F // X
    assert R == 4 and F % X == 0

    def on_device(base, lin, gout, ra, ea, rb, eb):
        T, D = base.shape
        rows, K = ra.shape
        half = rows // 2
        factor = 1.0 / math.sqrt(T * F * R)
        dma = pltpu.SemaphoreType.DMA
        vm = pltpu.VMEM
        any_spec = pl.BlockSpec(memory_space=pl.ANY)
        gli, gbase, grads = pl.pallas_call(
            functools.partial(kernel, F, R, factor),
            out_shape=(
                jax.ShapeDtypeStruct((T, D), BF16),
                jax.ShapeDtypeStruct((T, D), BF16),
                jax.ShapeDtypeStruct((4, rows, K), F32),
            ),
            in_specs=[any_spec] * 7,
            out_specs=[any_spec] * 3,
            scratch_shapes=[
                vm((T, D), BF16),
                vm((T, D), BF16),
                vm((2, 2, T, D), BF16),
                vm((2, 2, T, K), BF16),
                vm((2, T, D), BF16),
                vm((2, T, K), BF16),
                vm((4, D, K), BF16),
                vm((T, D), F32),
                vm((T, D), BF16),
                vm((T, D), BF16),
                vm((T, D), BF16),
                vm((2, D, K), F32),
                vm((4, rows, K), F32),
                vm((Z, 2, half, K), BF16),
                vm((Z, 2, half, K), BF16),
                vm((Z, 2, half, K), BF16),
                vm((Z, 2, half, K), BF16),
                vm((Z, half, K), BF16),
                vm((Z, half, K), BF16),
                vm((Z, half, K), BF16),
                vm((Z, half, K), BF16),
                vm((Z, 2, half, K), BF16),
                vm((2, Z, 2, half, K), BF16),
                vm((2, half, K), F32),
                vm((2, 2, half, K), BF16),
                dma((7,)),
                dma((3,)),
                dma((2, F, 2)),
                dma((2, F, 2)),
                dma((2, F, 2)),
                dma((2, F, 2)),
                dma((2, F, 2)),
                dma((2, F, 2)),
                dma((2, 2)),
                dma((2, 2)),
                dma((2, Z)),
                dma((2, Z)),
                dma((2, Z)),
                dma((2, Z)),
                dma((Z, 2)),
                dma((2, Z, 2)),
                dma((2, 2)),
                dma((2, 2)),
                dma((2, 2, 2)),
            ],
            compiler_params=pltpu.CompilerParams(
                collective_id=1, has_side_effects=True, vmem_limit_bytes=60 * 1024 * 1024
            ),
        )(base, lin, gout, ra, ea, rb, eb)
        return gli, gbase, grads[0], grads[1], grads[2], grads[3]

    both = P(("fsdp", "rep"), None)
    one = P("fsdp", None)
    return jax.shard_map(
        on_device,
        mesh=mesh,
        in_specs=(both, both, both, one, one, one, one),
        out_specs=(both, both, one, one, one, one),
        check_vma=False,
    )
```

time: 146 us -> 106 us (0.73)
  Pallas kernels: 140 us -> 99.2 us
    pallas_call x1, Pallas kernels: 140 us -> 99.2 us  [on_device(): pl.pallas_call(functools.partial(kernel, F, R, factor), out_shape=(jax.Sh...]
where the time goes in v2:
time: 106 us; the launch traced here: 105 us
  Pallas kernels  99.2 us (94%)
  local copies, waits for them, and re-layouts  5.52 us (5%)
    pallas_call x1, Pallas kernels, on_device(): pl.pallas_call(functools.partial(kernel, F, R, factor), out_shape=(jax.Sh...  99.2 us
    squeeze x1, local copies, waits for them, and re-layouts, on_device(): return (gli, gbase, grads[0], grads[1], grads[2], grads[3])  2.95 us
    unnamed x6, local copies, waits for them, and re-layouts  2.57 us

profile of v2, /device:TPU:1, one launch (start us, length us, event | category | flops | bytes accessed | tf_op | source)
XLA Modules:
  0.0 105.3 jit_solution(12086142359859293640)
XLA Ops:
  0.6 99.2 %shard_map.118 = (bf16[128,4096]{1,0:T(8,128)(2,1)}, bf16[128,4096]{1,0:T(8,128)(2,1)}, f32[4,512,256]{2,1,0:T(8,128)}) custom-call(bf16[128,4096]{1,0:T(8,128)(2,1)} %base_in.1, bf16[128,4096]{1,0:T(8,128)(2,1)} %lin_in.1, bf16[128,4096]{1,0:T(8,128)(2,1)} %gout_in.1, bf16[512,256]{1,0:T(8,128)(2,1)} %ra.1, bf16[512,256]{1,0:T(8,128)(2,1)} %ea.1, ...), custom_call_target="tpu_custom_call" | custom-call | tf_op jit(solution)/shard_map/pallas_call | solution.py:467
  99.8 0.0 copy-start.1
  99.8 2.9 %slice_bitcast_fusion = (f32[512,256]{1,0:T(8,128)}, f32[512,256]{1,0:T(8,128)}, f32[512,256]{1,0:T(8,128)}, f32[512,256]{1,0:T(8,128)}) fusion(f32[4,512,256]{2,1,0:T(8,128)} %get-tuple-element.11), kind=kLoop, calls=%fused_computation | loop fusion | bytes 4194304 | tf_op jit(solution)/shard_map/squeeze | solution.py:526
  102.8 0.0 copy-start
  102.8 0.0 copy-done.1
  102.8 1.0 copy.15
  103.7 0.6 copy-done
  104.4 1.0 copy.16
Async XLA Ops:
  99.8 3.0 %copy-start.1 = (bf16[128,4096]{1,0:T(8,128)(2,1)S(1)}, bf16[128,4096]{1,0:T(8,128)(2,1)}, u32[]{:S(2)}) copy-start(bf16[128,4096]{1,0:T(8,128)(2,1)} %get-tuple-element.22) | copy-start | bytes 3145732
  102.8 1.6 %copy-start = (bf16[128,4096]{1,0:T(8,128)(2,1)S(1)}, bf16[128,4096]{1,0:T(8,128)(2,1)}, u32[]{:S(2)}) copy-start(bf16[128,4096]{1,0:T(8,128)(2,1)} %get-tuple-element.23) | copy-start | bytes 3145732

commit v3 on v2

--- a/solution.py
+++ b/solution.py
@@ -28,7 +28,6 @@
 def kernel(
     F,
     R,
-    factor,
     base_in,
     lin_in,
     gout_in,
@@ -58,8 +57,6 @@
     x1_recv,
     x2_send,
     x2_recv,
-    y2_send,
-    y2_recv,
     z_send,
     z_recv,
     last_sum,
@@ -77,7 +74,6 @@
     y1_sem,
     x1_sem,
     x2_sem,
-    y2_sem,
     zs_sem,
     zr_sem,
     y_ssem,
@@ -129,6 +125,19 @@
     for copy in loads[:4]:
         copy.wait()
 
+    def push(src, dst, sems, target):
+        copy = pltpu.make_async_remote_copy(
+            src_ref=src, dst_ref=dst, send_sem=sems[0], recv_sem=sems[1],
+            device_id=target, device_id_type=MESH,
+        )
+        copy.start()
+        return copy
+
+    swaps = []
+
+    def swap(src, dst, sem, k):
+        swaps.append(push(src.at[1 - c, k], dst.at[k], (sem.at[0, k], sem.at[1, k]), mate))
+
     sent = []
 
     def guarded(cond, action):
@@ -239,6 +248,7 @@
         cols = pl.ds(pl.multiple_of(t * tile, tile), tile)
         own[1, 1, :, cols] = (gout[:, cols].astype(F32) * base[:, cols].astype(F32)).astype(BF16)
 
+    swap(own, peer_wide, pw_sem, 1 - c)
     for d in range(1, Z + 2):
         if d < Z:
             stage_line(d)
@@ -276,27 +286,12 @@
         gmid[:, cols] = passed
         own[0, 1, :, cols] = (passed.astype(F32) * wide).astype(BF16)
 
+    swap(own, peer_wide, pw_sem, c)
     nar[1, 1] = dot_nn(own[1, 0], full[2]).astype(BF16)
     nar[0, 0] = dot_nn(own[0, 1], full[1]).astype(BF16)
 
-    swaps = []
     for k in range(2):
-        for src, dst, sem in ((own, peer_wide, pw_sem), (nar, peer_nar, pn_sem)):
-            copy = pltpu.make_async_remote_copy(
-                src_ref=src.at[1 - c, k], dst_ref=dst.at[k], send_sem=sem.at[0, k],
-                recv_sem=sem.at[1, k], device_id=mate, device_id_type=MESH,
-            )
-            copy.start()
-            swaps.append(copy)
-
-    def push(src, dst, sems, target):
-        copy = pltpu.make_async_remote_copy(
-            src_ref=src, dst_ref=dst, send_sem=sems[0], recv_sem=sems[1],
-            device_id=target, device_id_type=MESH,
-        )
-        copy.start()
-        return copy
-
+        swap(nar, peer_nar, pn_sem, k)
     for copy in swaps:
         copy.wait()
     level_rows = X * rows
@@ -342,21 +337,18 @@
         one.wait_recv()
         x2_send[o] = (mine(y, o, xo, 0) + y1_recv[o, xo].astype(F32)).astype(BF16)
         three = push(x2_send.at[o], x2_recv.at[o], (x2_sem.at[0, o], x2_sem.at[1, o]), across)
-        two.wait_recv()
-        y2_send[o] = (mine(yo, o, x, 1) + x1_recv[o, yo].astype(F32)).astype(BF16)
-        four = push(y2_send.at[o], y2_recv.at[o], (y2_sem.at[0, o], y2_sem.at[1, o]), twin)
-        waits.extend((three, four))
-        sums[i] = (three, four)
-
-    def level_sum(o, h):
-        if h == 0:
+        waits.append(three)
+        sums[i] = (two, None, three)
+
+    def level_sum(o, n):
+        if n == 2:
             return mine(y, o, x, 0) + y1_recv[o, x].astype(F32) + x2_recv[o].astype(F32)
-        return mine(y, o, x, 1) + x1_recv[o, y].astype(F32) + y2_recv[o].astype(F32)
-
-    def line(o, h, way, target):
+        return mine(n, o, x, 1) + x1_recv[o, n].astype(F32)
+
+    def line(o, n, way, target):
         return pltpu.make_async_remote_copy(
-            src_ref=z_send.at[o, h], dst_ref=z_recv.at[way, o, h], send_sem=zs_sem.at[o, h],
-            recv_sem=zr_sem.at[way, o, h], device_id=target, device_id_type=MESH,
+            src_ref=z_send.at[o, n], dst_ref=z_recv.at[way, o, n], send_sem=zs_sem.at[o, n],
+            recv_sem=zr_sem.at[way, o, n], device_id=target, device_id_type=MESH,
         )
 
     def third(i):
@@ -364,19 +356,20 @@
         way = jnp.where(o > z, 0, 1)
         target = dev((z + 1 - 2 * way) * X + x, r)
         fed = jnp.where(o > z, z, Z - 1 - z) > 0
-        for h in range(2):
-            sums[i][h].wait_recv()
-            value = level_sum(o, h)
-            copy = line(o, h, way, target)
+        for n in range(3):
+            if sums[i][n] is not None:
+                sums[i][n].wait_recv()
+            value = level_sum(o, n)
+            copy = line(o, n, way, target)
 
             @pl.when(fed)
             def _():
                 copy.wait_recv()
-                z_send[o, h] = (value + z_recv[way, o, h].astype(F32)).astype(BF16)
+                z_send[o, n] = (value + z_recv[way, o, n].astype(F32)).astype(BF16)
 
             @pl.when(jnp.logical_not(fed))
             def _():
-                z_send[o, h] = value.astype(BF16)
+                z_send[o, n] = value.astype(BF16)
 
             copy.start()
             waits.append(copy)
@@ -408,33 +401,36 @@
             third(i - 2)
 
     hy = []
-    for h in range(2):
-        sums[Z - 1][h].wait_recv()
-        last_sum[h] = level_sum(z, h)
+    for n in range(3):
+        if sums[Z - 1][n] is not None:
+            sums[Z - 1][n].wait_recv()
+        last_sum[n] = level_sum(z, n)
         for way, cond in ((0, not_bottom), (1, not_top)):
 
             @pl.when(cond)
             def _():
-                line(z, h, way, across).wait_recv()
-                last_sum[h] = last_sum[h] + z_recv[way, z, h].astype(F32)
-
-        fin[y, h] = last_sum[h].astype(BF16)
-        hy.append(push(fin.at[y, h], fin.at[y, h], (y_ssem.at[y, h], y_rsem.at[y, h]), twin))
+                line(z, n, way, across).wait_recv()
+                last_sum[n] = last_sum[n] + z_recv[way, z, n].astype(F32)
+
+        fin[y, n] = last_sum[n].astype(BF16)
+        hy.append(push(fin.at[y, n], fin.at[y, n], (y_ssem.at[y, n], y_rsem.at[y, n]), twin))
     hg = []
 
-    def hand_over(k, h):
-        grads[2 * c + k, pl.ds(h * half, half), :] = fin[k, h].astype(F32) * factor
+    def hand_over(k, h, value):
+        grads[2 * c + k, pl.ds(h * half, half), :] = value
         ref = grads.at[2 * c + k, pl.ds(h * half, half), :]
         hg.append(push(ref, ref, (g_sem.at[0, k, h], g_sem.at[1, k, h]), mate))
 
-    for h in range(2):
-        hand_over(y, h)
-    for h in range(2):
+    hand_over(y, 0, fin[y, 2])
+    for n in range(3):
         pltpu.make_async_remote_copy(
-            src_ref=fin.at[yo, h], dst_ref=fin.at[yo, h], send_sem=y_ssem.at[yo, h],
-            recv_sem=y_rsem.at[yo, h], device_id=twin, device_id_type=MESH,
+            src_ref=fin.at[yo, n], dst_ref=fin.at[yo, n], send_sem=y_ssem.at[yo, n],
+            recv_sem=y_rsem.at[yo, n], device_id=twin, device_id_type=MESH,
         ).wait_recv()
-        hand_over(yo, h)
+        if n < 2:
+            hand_over(n, 1, (fin[0, n].astype(F32) + fin[1, n].astype(F32)).astype(BF16))
+        else:
+            hand_over(yo, 0, fin[yo, 2])
     for k in range(2):
         for h in range(2):
             ref = grads.at[2 * (1 - c) + k, pl.ds(h * half, half), :]
@@ -465,11 +461,11 @@
         vm = pltpu.VMEM
         any_spec = pl.BlockSpec(memory_space=pl.ANY)
         gli, gbase, grads = pl.pallas_call(
-            functools.partial(kernel, F, R, factor),
+            functools.partial(kernel, F, R),
             out_shape=(
                 jax.ShapeDtypeStruct((T, D), BF16),
                 jax.ShapeDtypeStruct((T, D), BF16),
-                jax.ShapeDtypeStruct((4, rows, K), F32),
+                jax.ShapeDtypeStruct((4, rows, K), BF16),
             ),
             in_specs=[any_spec] * 7,
             out_specs=[any_spec] * 3,
@@ -486,19 +482,17 @@
                 vm((T, D), BF16),
                 vm((T, D), BF16),
                 vm((2, D, K), F32),
-                vm((4, rows, K), F32),
+                vm((4, rows, K), BF16),
                 vm((Z, 2, half, K), BF16),
                 vm((Z, 2, half, K), BF16),
                 vm((Z, 2, half, K), BF16),
                 vm((Z, 2, half, K), BF16),
                 vm((Z, half, K), BF16),
                 vm((Z, half, K), BF16),
-                vm((Z, half, K), BF16),
-                vm((Z, half, K), BF16),
-                vm((Z, 2, half, K), BF16),
-                vm((2, Z, 2, half, K), BF16),
-                vm((2, half, K), F32),
-                vm((2, 2, half, K), BF16),
+                vm((Z, 3, half, K), BF16),
+                vm((2, Z, 3, half, K), BF16),
+                vm((3, half, K), F32),
+                vm((2, 3, half, K), BF16),
                 dma((7,)),
                 dma((3,)),
                 dma((2, F, 2)),
@@ -512,18 +506,18 @@
                 dma((2, Z)),
                 dma((2, Z)),
                 dma((2, Z)),
-                dma((2, Z)),
-                dma((Z, 2)),
-                dma((2, Z, 2)),
-                dma((2, 2)),
-                dma((2, 2)),
+                dma((Z, 3)),
+                dma((2, Z, 3)),
+                dma((2, 3)),
+                dma((2, 3)),
                 dma((2, 2, 2)),
             ],
             compiler_params=pltpu.CompilerParams(
                 collective_id=1, has_side_effects=True, vmem_limit_bytes=60 * 1024 * 1024
             ),
         )(base, lin, gout, ra, ea, rb, eb)
-        return gli, gbase, grads[0], grads[1], grads[2], grads[3]
+        scaled = [grads[w].astype(F32) * factor for w in range(4)]
+        return (gli, gbase, *scaled)
 
     both = P(("fsdp", "rep"), None)
     one = P("fsdp", None)

time: 106 us -> 104 us (0.981)
  local copies, waits for them, and re-layouts: 5.52 us -> 2.58 us
  other arithmetic: 0 us -> 2.63 us
  Pallas kernels: 99.2 us -> 97.5 us
    squeeze x1 -> x0, local copies, waits for them, and re-layouts: 2.95 us -> none  [on_device(): return (gli, gbase, grads[0], grads[1], grads[2], grads[3])]
    mul x0 -> x1, other arithmetic: none -> 2.63 us  [on_device(): scaled = [grads[w].astype(F32) * factor for w in range(4)]]
    pallas_call x1, Pallas kernels: 99.2 us -> 97.5 us  [on_device(): pl.pallas_call(functools.partial(kernel, F, R), out_shape=(jax.ShapeDtype...]
where the time goes in v3:
time: 104 us; the launch traced here: 103 us
  Pallas kernels  97.5 us (94%)
  other arithmetic  2.63 us (3%)
  local copies, waits for them, and re-layouts  2.58 us (2%)
    pallas_call x1, Pallas kernels, on_device(): pl.pallas_call(functools.partial(kernel, F, R), out_shape=(jax.ShapeDtype...  97.5 us
    mul x1, other arithmetic, on_device(): scaled = [grads[w].astype(F32) * factor for w in range(4)]  2.63 us
    unnamed x6, local copies, waits for them, and re-layouts  2.58 us

profile of v3, /device:TPU:1, one launch (start us, length us, event | category | flops | bytes accessed | tf_op | source)
XLA Modules:
  0.0 103.3 jit_solution(1883395561929235876)
XLA Ops:
  0.6 97.5 %shard_map.118 = (bf16[128,4096]{1,0:T(8,128)(2,1)}, bf16[128,4096]{1,0:T(8,128)(2,1)}, bf16[4,512,256]{2,1,0:T(8,128)(2,1)}) custom-call(bf16[128,4096]{1,0:T(8,128)(2,1)} %base_in.1, bf16[128,4096]{1,0:T(8,128)(2,1)} %lin_in.1, bf16[128,4096]{1,0:T(8,128)(2,1)} %gout_in.1, bf16[512,256]{1,0:T(8,128)(2,1)} %ra.1, bf16[512,256]{1,0:T(8,128)(2,1)} %ea.1, ...), custom_call_target="tpu_custom_call" | custom-call | tf_op jit(solution)/shard_map/pallas_call | solution.py:463
  98.1 0.0 copy-start.1
  98.1 2.6 %multiply_bitcast_fusion = (f32[512,256]{1,0:T(8,128)}, f32[512,256]{1,0:T(8,128)}, f32[512,256]{1,0:T(8,128)}, f32[512,256]{1,0:T(8,128)}) fusion(bf16[4,512,256]{2,1,0:T(8,128)(2,1)} %get-tuple-element.11), kind=kLoop, calls=%fused_computation | loop fusion | flops 1048576 | bytes 3145728 | tf_op jit(solution)/shard_map/mul | solution.py:519
  100.7 0.0 copy-done.1
  100.7 0.0 copy-start
  100.7 1.0 copy.15
  101.7 0.6 copy-done
  102.3 1.0 copy.16
Async XLA Ops:
  98.1 2.6 %copy-start.1 = (bf16[128,4096]{1,0:T(8,128)(2,1)S(1)}, bf16[128,4096]{1,0:T(8,128)(2,1)}, u32[]{:S(2)}) copy-start(bf16[128,4096]{1,0:T(8,128)(2,1)} %get-tuple-element.22) | copy-start | bytes 3145732
  100.7 1.6 %copy-start = (bf16[128,4096]{1,0:T(8,128)(2,1)S(1)}, bf16[128,4096]{1,0:T(8,128)(2,1)}, u32[]{:S(2)}) copy-start(bf16[128,4096]{1,0:T(8,128)(2,1)} %get-tuple-element.23) | copy-start | bytes 3145732

commit v4 on v3

--- a/solution.py
+++ b/solution.py
@@ -165,9 +165,9 @@
         guarded(cond, copy.start)
         sent.append((cond, copy))
 
-    def zsend(cond, zz, h, upward):
-        o = slot(zz, x)
-        relay(cond, y, zz, x, h, ag_z.at[upward, o, h], ag_recv.at[y, o, h], up if upward else down)
+    def zsend(cond, zz, xx, h, upward):
+        o = slot(zz, xx)
+        relay(cond, y, zz, xx, h, ag_z.at[upward, o, h], ag_recv.at[y, o, h], up if upward else down)
 
     def xsend(cond, k, zz, h):
         o = slot(zz, x)
@@ -200,34 +200,46 @@
     not_top, not_bottom = z < Z - 1, z > 0
     yo = 1 - y
 
+    def along(d, cond, zz, xx, h, upward):
+        if d == 0:
+            zsend(not_top, zz, xx, h, 1)
+            zsend(not_bottom, zz, xx, h, 0)
+        elif d < Z - 1:
+            zsend(also(cond, not_top if upward else not_bottom), zz, xx, h, 1 if upward else 0)
+
     def stage_line(d):
-        for h in range(2):
+        for h in (1, 0):
             for zz, cond, upward in levels(d):
-                if d == 0:
-                    zsend(not_top, zz, h, 1)
-                    zsend(not_bottom, zz, h, 0)
-                else:
+                if d > 0:
                     arrive(cond, y, zz, x, h)
-                    if d < Z - 1:
-                        zsend(also(cond, not_top if upward else not_bottom), zz, h, 1 if upward else 0)
-                xsend(cond, y, zz, h)
-                if d == 0:
-                    if h == 1:
-                        xsend(cond, yo, zz, h)
-                else:
+                along(d, cond, zz, x, h, upward)
+                if d == 0 or h == 0:
+                    xsend(cond, y, zz, h)
+                if d > 0:
                     ysend(cond, zz, x, h)
                     dsend(cond, y, zz, x, h)
+        if d == 0:
+            xsend(None, yo, z, 1)
+
+    def stage_other(d):
+        for zz, cond, upward in levels(d):
+            arrive(cond, y, zz, xo, 1)
+            along(d, cond, zz, xo, 1, upward)
+            if d > 1:
+                ysend(cond, zz, xo, 1)
+            dsend(cond, y, zz, xo, 1)
 
     def stage_side(d):
-        for h in range(2):
-            for zz, cond, _ in levels(d):
-                arrive(cond, y, zz, xo, h)
-                if h == 0:
-                    ysend(cond, zz, xo, h)
-                dsend(cond, y, zz, xo, h)
-                if d > 0:
+        for zz, cond, _ in levels(d):
+            arrive(cond, y, zz, xo, 0)
+            if d == 0:
+                ysend(cond, zz, xo, 0)
+            dsend(cond, y, zz, xo, 0)
+        if d > 0:
+            for h in (1, 0):
+                for zz, cond, _ in levels(d):
                     arrive(cond, yo, zz, x, h)
-                    if h == 1:
+                    if h == 0 or d == 1:
                         xsend(cond, yo, zz, h)
                     dsend(cond, yo, zz, x, h)
 
@@ -250,8 +262,12 @@
 
     swap(own, peer_wide, pw_sem, 1 - c)
     for d in range(1, Z + 2):
+        if d == 1:
+            stage_other(0)
         if d < Z:
             stage_line(d)
+        if d > 1 and d - 1 < Z:
+            stage_other(d - 1)
         stage_side(d - 1)
         stage_corner(d - 2)
     for d in range(Z):
@@ -386,19 +402,22 @@
             gli[:, cols] = (held + dot_nt(nar[0, 0], full[0, cols, :])).astype(BF16)
 
     outs = []
-    for i in range(Z + 1):
-        if i < Z:
-            first(i)
-        if i == min(1, Z - 1):
-            others()
-            for n, (src, dst) in enumerate(((gli, gli_out), (gbase, gbase_out))):
-                copy = pltpu.make_async_copy(src, dst, out_sem.at[n])
-                copy.start()
-                outs.append(copy)
-        if 1 <= i:
+    for i in range(Z - 1):
+        first(i)
+        if i > 0:
             second(i - 1)
-        if 2 <= i:
-            third(i - 2)
+            if i > 1:
+                third(i - 2)
+    second(Z - 2)
+    first(Z - 1)
+    others()
+    for n, (src, dst) in enumerate(((gli, gli_out), (gbase, gbase_out))):
+        copy = pltpu.make_async_copy(src, dst, out_sem.at[n])
+        copy.start()
+        outs.append(copy)
+    second(Z - 1)
+    for i in range(max(Z - 3, 0), Z - 1):
+        third(i)
 
     hy = []
     for n in range(3):

time: 104 us -> 106 us (1.019)
  Pallas kernels: 97.5 us -> 99.6 us
    pallas_call x1, Pallas kernels: 97.5 us -> 99.6 us  [on_device(): pl.pallas_call(functools.partial(kernel, F, R), out_shape=(jax.ShapeDtype...]
where the time goes in v4:
time: 106 us; the launch traced here: 105 us
  Pallas kernels  99.6 us (94%)
  other arithmetic  2.63 us (2%)
  local copies, waits for them, and re-layouts  2.58 us (2%)
    pallas_call x1, Pallas kernels, on_device(): pl.pallas_call(functools.partial(kernel, F, R), out_shape=(jax.ShapeDtype...  99.6 us
    mul x1, other arithmetic, on_device(): scaled = [grads[w].astype(F32) * factor for w in range(4)]  2.63 us
    unnamed x6, local copies, waits for them, and re-layouts  2.58 us

profile of v4, /device:TPU:1, one launch (start us, length us, event | category | flops | bytes accessed | tf_op | source)
XLA Modules:
  0.0 105.5 jit_solution(15241137051360329073)
XLA Ops:
  0.6 99.6 %shard_map.118 = (bf16[128,4096]{1,0:T(8,128)(2,1)}, bf16[128,4096]{1,0:T(8,128)(2,1)}, bf16[4,512,256]{2,1,0:T(8,128)(2,1)}) custom-call(bf16[128,4096]{1,0:T(8,128)(2,1)} %base_in.1, bf16[128,4096]{1,0:T(8,128)(2,1)} %lin_in.1, bf16[128,4096]{1,0:T(8,128)(2,1)} %gout_in.1, bf16[512,256]{1,0:T(8,128)(2,1)} %ra.1, bf16[512,256]{1,0:T(8,128)(2,1)} %ea.1, ...), custom_call_target="tpu_custom_call" | custom-call | tf_op jit(solution)/shard_map/pallas_call | solution.py:482
  100.3 0.0 copy-start.1
  100.3 2.6 %multiply_bitcast_fusion = (f32[512,256]{1,0:T(8,128)}, f32[512,256]{1,0:T(8,128)}, f32[512,256]{1,0:T(8,128)}, f32[512,256]{1,0:T(8,128)}) fusion(bf16[4,512,256]{2,1,0:T(8,128)(2,1)} %get-tuple-element.11), kind=kLoop, calls=%fused_computation | loop fusion | flops 1048576 | bytes 3145728 | tf_op jit(solution)/shard_map/mul | solution.py:538
  102.9 0.0 copy-done.1
  102.9 0.0 copy-start
  102.9 1.0 copy.15
  103.9 0.6 copy-done
  104.5 1.0 copy.16
Async XLA Ops:
  100.3 2.6 %copy-start.1 = (bf16[128,4096]{1,0:T(8,128)(2,1)S(1)}, bf16[128,4096]{1,0:T(8,128)(2,1)}, u32[]{:S(2)}) copy-start(bf16[128,4096]{1,0:T(8,128)(2,1)} %get-tuple-element.22) | copy-start | bytes 3145732
  102.9 1.6 %copy-start = (bf16[128,4096]{1,0:T(8,128)(2,1)S(1)}, bf16[128,4096]{1,0:T(8,128)(2,1)}, u32[]{:S(2)}) copy-start(bf16[128,4096]{1,0:T(8,128)(2,1)} %get-tuple-element.23) | copy-start | bytes 3145732

commit v5 on v3

--- a/solution.py
+++ b/solution.py
@@ -386,19 +386,22 @@
             gli[:, cols] = (held + dot_nt(nar[0, 0], full[0, cols, :])).astype(BF16)
 
     outs = []
-    for i in range(Z + 1):
-        if i < Z:
-            first(i)
-        if i == min(1, Z - 1):
-            others()
-            for n, (src, dst) in enumerate(((gli, gli_out), (gbase, gbase_out))):
-                copy = pltpu.make_async_copy(src, dst, out_sem.at[n])
-                copy.start()
-                outs.append(copy)
-        if 1 <= i:
+    for i in range(Z - 1):
+        first(i)
+        if i > 0:
             second(i - 1)
-        if 2 <= i:
-            third(i - 2)
+            if i > 1:
+                third(i - 2)
+    second(Z - 2)
+    first(Z - 1)
+    others()
+    for n, (src, dst) in enumerate(((gli, gli_out), (gbase, gbase_out))):
+        copy = pltpu.make_async_copy(src, dst, out_sem.at[n])
+        copy.start()
+        outs.append(copy)
+    second(Z - 1)
+    for i in range(max(Z - 3, 0), Z - 1):
+        third(i)
 
     hy = []
     for n in range(3):

time: 104 us -> 108 us (1.038)
  Pallas kernels: 97.5 us -> 102 us
    pallas_call x1, Pallas kernels: 97.5 us -> 102 us  [on_device(): pl.pallas_call(functools.partial(kernel, F, R), out_shape=(jax.ShapeDtype...]
where the time goes in v5:
time: 108 us
  Pallas kernels  102 us (94%)
  other arithmetic  2.63 us (2%)
  local copies, waits for them, and re-layouts  2.58 us (2%)
    pallas_call x1, Pallas kernels, on_device(): pl.pallas_call(functools.partial(kernel, F, R), out_shape=(jax.ShapeDtype...  102 us
    mul x1, other arithmetic, on_device(): scaled = [grads[w].astype(F32) * factor for w in range(4)]  2.63 us
    unnamed x6, local copies, waits for them, and re-layouts  2.58 us

profile of v5, /device:TPU:1, one launch (start us, length us, event | category | flops | bytes accessed | tf_op | source)
XLA Modules:
  0.0 108.3 jit_solution(3816213495332417052)
XLA Ops:
  0.6 102.4 %shard_map.118 = (bf16[128,4096]{1,0:T(8,128)(2,1)}, bf16[128,4096]{1,0:T(8,128)(2,1)}, bf16[4,512,256]{2,1,0:T(8,128)(2,1)}) custom-call(bf16[128,4096]{1,0:T(8,128)(2,1)} %base_in.1, bf16[128,4096]{1,0:T(8,128)(2,1)} %lin_in.1, bf16[128,4096]{1,0:T(8,128)(2,1)} %gout_in.1, bf16[512,256]{1,0:T(8,128)(2,1)} %ra.1, bf16[512,256]{1,0:T(8,128)(2,1)} %ea.1, ...), custom_call_target="tpu_custom_call" | custom-call | tf_op jit(solution)/shard_map/pallas_call | solution.py:466
  103.0 0.0 copy-start.1
  103.0 2.6 %multiply_bitcast_fusion = (f32[512,256]{1,0:T(8,128)}, f32[512,256]{1,0:T(8,128)}, f32[512,256]{1,0:T(8,128)}, f32[512,256]{1,0:T(8,128)}) fusion(bf16[4,512,256]{2,1,0:T(8,128)(2,1)} %get-tuple-element.11), kind=kLoop, calls=%fused_computation | loop fusion | flops 1048576 | bytes 3145728 | tf_op jit(solution)/shard_map/mul | solution.py:522
  105.7 0.0 copy-done.1
  105.7 0.0 copy-start
  105.7 1.0 copy.15
  106.7 0.6 copy-done
  107.3 1.0 copy.16
Async XLA Ops:
  103.0 2.6 %copy-start.1 = (bf16[128,4096]{1,0:T(8,128)(2,1)S(1)}, bf16[128,4096]{1,0:T(8,128)(2,1)}, u32[]{:S(2)}) copy-start(bf16[128,4096]{1,0:T(8,128)(2,1)} %get-tuple-element.22) | copy-start | bytes 3145732
  105.7 1.6 %copy-start = (bf16[128,4096]{1,0:T(8,128)(2,1)S(1)}, bf16[128,4096]{1,0:T(8,128)(2,1)}, u32[]{:S(2)}) copy-start(bf16[128,4096]{1,0:T(8,128)(2,1)} %get-tuple-element.23) | copy-start | bytes 3145732
